TPU v7x, 32 devices: a whole 2x2x4 slice. The times are simulated.
32 devices in a mesh: px: 4 (over x, core), py: 2 (over y), pz: 4 (over z).
Axes of the slice: x: 2, y: 2, z: 4, core: 2. Of those that a mesh axis runs over, the one named last changes fastest.
Arguments:
- control_values: float32 [28, 14, 28, 512], P('px', 'py', 'pz'), may hold values from -6 to 6
- metric_diag: float32 [3, 32, 512], P(None, 'px', ('py', 'pz')), may hold values from 0.5 to 2
- metric_off: float32 [3, 32, 512], P(None, 'px', ('py', 'pz')), may hold values from -0.2 to 0.2
- mass_weight: float32 [32, 512], P('px', ('py', 'pz')), may hold values from 0.5 to 2
- orient: int32 [4, 2, 4, 3], P('px', 'py', 'pz'), may hold values from 0 to 1
Outputs:
- stiffness_out: float32 [28, 14, 28, 512], P('px', 'py', 'pz')
- mass_out: float32 [28, 14, 28, 512], P('px', 'py', 'pz')
All inputs are finite; a program needn't handle non-finite values.
Results may differ from a plain program's by a relative error of at most 0.0003.
Values sent between devices are 32-bit elements; how exact they have to be, the bound alone decides.
A program may use at most 64 MiB of HBM per device.

v0:
```python
import functools
import heapq
import math

import jax
import jax.numpy as jnp
import numpy as np
from jax import lax
from jax.experimental import pallas as pl
from jax.experimental.pallas import tpu as pltpu
from jax.sharding import PartitionSpec as P

LANES = 128
ROWS = 8
AXES = ("px", "py", "pz")


def spline_tables(elements):
    knot_row = np.concatenate(
        [np.zeros(3), np.arange(elements + 1) * 1.0, np.full(3, float(elements))]
    )
    offsets = np.array([0.5 - 0.5 / math.sqrt(3.0), 0.5 + 0.5 / math.sqrt(3.0)])
    points = (np.arange(elements)[:, None] + offsets[None, :]).reshape(-1)
    intervals = np.repeat(np.arange(elements), 2) + 3
    current = np.zeros((points.size, knot_row.size - 1))
    current[np.arange(points.size), intervals] = 1.0
    previous = current
    for degree in range(1, 4):
        columns = knot_row.size - 1 - degree
        updated = np.zeros((points.size, columns))
        for i in range(columns):
            lower_gap = knot_row[i + degree] - knot_row[i]
            upper_gap = knot_row[i + degree + 1] - knot_row[i + 1]
            if lower_gap > 0:
                updated[:, i] += (points - knot_row[i]) / lower_gap * current[:, i]
            if upper_gap > 0:
                updated[:, i] += (knot_row[i + degree + 1] - points) / upper_gap * current[:, i + 1]
        previous = current
        current = updated
    slopes = np.zeros(current.shape)
    for i in range(current.shape[1]):
        lower_gap = knot_row[i + 3] - knot_row[i]
        upper_gap = knot_row[i + 4] - knot_row[i + 1]
        if lower_gap > 0:
            slopes[:, i] += 3.0 / lower_gap * previous[:, i]
        if upper_gap > 0:
            slopes[:, i] -= 3.0 / upper_gap * previous[:, i + 1]
    return (current.astype(np.float32), slopes.astype(np.float32))


def split(x):
    high = x.astype(jnp.bfloat16)
    return high, (x - high.astype(jnp.float32)).astype(jnp.bfloat16)


def split_table(table):
    high = table.astype(jnp.bfloat16)
    low = (table - high.astype(np.float32)).astype(jnp.bfloat16)
    return np.asarray(high), np.asarray(low)


def plane_tables(values, slopes):
    quad, ctrl = values.shape
    wide = np.zeros((quad, ROWS), np.float64)
    tall = np.zeros((quad, ROWS), np.float64)
    wide[:, :ctrl] = values
    tall[:, :ctrl] = slopes
    fields = [np.kron(wide, wide), np.kron(tall, wide), np.kron(wide, tall)]
    forward = np.concatenate(fields, 0).astype(np.float32)
    high, low = split_table(forward)
    forward = np.concatenate([high, high, low], 1)
    backward = []
    size = ctrl * ROWS
    for flip_y in range(2):
        for flip_z in range(2):
            rows = np.full(size, -1)
            for j in range(ctrl):
                for k in range(ctrl):
                    jj = ctrl - 1 - j if flip_y else j
                    kk = ctrl - 1 - k if flip_z else k
                    rows[j * ROWS + k] = jj * ROWS + kk
            back = [np.where(rows[:, None] >= 0, f.T[rows], 0.0) for f in fields]
            none = np.zeros_like(back[0])
            stiff = np.concatenate([back[0], back[1], back[2], none], 1)
            mass = np.concatenate([none, none, none, back[0]], 1)
            backward.append(np.concatenate([stiff, mass], 0).astype(np.float32))
    return forward, np.stack(backward)


def make_copies(orders, zsend, bufs, state, send_sem, recv_sem, nbrs, c, stage):
    ctrl = state.shape[2]
    d = orders[c % len(orders)][stage]
    result = []
    for side in range(2):
        e = side * (ctrl - 1)
        if d == 0:
            plane = state.at[c, :, e]
        elif d == 1:
            plane = state.at[c, :, :, e * ROWS : e * ROWS + ctrl]
        else:
            plane = zsend.at[c, side]
        result.append(
            pltpu.make_async_remote_copy(
                src_ref=plane,
                dst_ref=bufs[d].at[c, 1 - side],
                send_sem=send_sem.at[c, d, side],
                recv_sem=recv_sem.at[c, d, 1 - side],
                device_id={AXES[d]: nbrs[d][side]},
                device_id_type=pl.DeviceIdType.MESH,
            )
        )
    return result


def patch_kernel(
    values, slopes, orient, u_hbm, diag_ref, off_ref, weight_ref, fwd_ref, bwd_ref,
    stiff_hbm, mass_hbm,
    ubuf, upad, square, coef, fields, back, table, state, xbuf, ybuf, zbuf, zsend, turned,
    u_sem, out_sem, send_sem, recv_sem,
):
    quad, ctrl = values.shape
    vecs = u_hbm.shape[3]
    halves, width = ubuf.shape[0], ubuf.shape[4]
    chunks = vecs // LANES
    per_half = width // LANES
    points = quad * quad
    size = ctrl * ROWS
    bufs = (xbuf, ybuf, zbuf)

    loads = [
        pltpu.make_async_copy(
            u_hbm.at[:, :, :, h * width : (h + 1) * width], ubuf.at[h], u_sem.at[h]
        )
        for h in range(halves)
    ]
    for load in loads:
        load.start()

    nbrs = []
    for axis in AXES:
        count, me = lax.axis_size(axis), lax.axis_index(axis)
        nbrs.append((lax.rem(me + count - 1, count), lax.rem(me + 1, count)))
    barrier = pltpu.get_barrier_semaphore()
    for d in range(3):
        for side in range(2):
            pl.semaphore_signal(
                barrier,
                inc=1,
                device_id={AXES[d]: nbrs[d][side]},
                device_id_type=pl.DeviceIdType.MESH,
            )

    upad[...] = jnp.zeros_like(upad)
    square[...] = jnp.zeros_like(square)
    for s in range(3):
        square[s * quad : (s + 1) * quad, 0:points] = diag_ref[s]
        square[(3 + s) * quad : (4 + s) * quad, 0:points] = off_ref[s]
    square[6 * quad : 7 * quad, 0:points] = weight_ref[...]
    across = square[...].T
    for c in range(7 * quad):
        coef[c] = jnp.broadcast_to(across[0:points, c : c + 1], (points, LANES))

    def flips(shape):
        return [jnp.full(shape, orient[d], jnp.int32) == 1 for d in range(3)]

    _, flip_y, flip_z = flips(bwd_ref.shape[1:])
    high, low = split(
        jnp.where(
            flip_y,
            jnp.where(flip_z, bwd_ref[3], bwd_ref[2]),
            jnp.where(flip_z, bwd_ref[1], bwd_ref[0]),
        )
    )
    table[0 : 2 * size] = high
    table[2 * size : 4 * size] = low

    def operate(h):
        for i in range(ctrl):
            upad[i % 2, 0:ctrl, 0:ctrl, :] = ubuf[h, i]
            high, low = split(upad[i % 2].reshape(ROWS * ROWS, width))
            stacked = jnp.concatenate([high, low, high], axis=0)
            fields[i] = jnp.dot(fwd_ref[...], stacked, preferred_element_type=jnp.float32)

        @pl.loop(0, quad)
        def _(b):
            row = pl.multiple_of(b * ROWS, ROWS)
            for l in range(per_half):
                lanes = slice(l * LANES, (l + 1) * LANES)
                part = [
                    [fields[i, pl.ds(f * points + row, ROWS), lanes] for f in range(3)]
                    for i in range(ctrl)
                ]
                acc = [[None] * ctrl for _ in range(4)]
                for q in range(quad):
                    near = [i for i in range(ctrl) if values[q, i] != 0.0 or slopes[q, i] != 0.0]
                    v = {i: float(values[q, i]) for i in near}
                    s = {i: float(slopes[q, i]) for i in near}
                    g1 = sum(s[i] * part[i][0] for i in near)
                    p = sum(v[i] * part[i][0] for i in near)
                    g2 = sum(v[i] * part[i][1] for i in near)
                    g3 = sum(v[i] * part[i][2] for i in near)
                    d = [coef[t * quad + q, pl.ds(row, ROWS), :] for t in range(7)]
                    flux = [
                        d[0] * g1 + d[3] * g2 + d[4] * g3,
                        d[3] * g1 + d[1] * g2 + d[5] * g3,
                        d[4] * g1 + d[5] * g2 + d[2] * g3,
                        d[6] * p,
                    ]
                    for f in range(4):
                        for i in near:
                            term = (s[i] if f == 0 else v[i]) * flux[f]
                            acc[f][i] = term if acc[f][i] is None else acc[f][i] + term
                for f in range(4):
                    for i in range(ctrl):
                        back[i, pl.ds(f * points + row, ROWS), lanes] = acc[f][i]

        flip = flips((4 * points, width))[0]
        for i in range(ctrl):
            high, low = split(jnp.where(flip, back[ctrl - 1 - i], back[i]))
            both = jnp.dot(table[...], high, preferred_element_type=jnp.float32)
            rest = jnp.dot(table[0 : 2 * size], low, preferred_element_type=jnp.float32)
            total = both[0 : 2 * size] + both[2 * size : 4 * size] + rest
            for f in range(2):
                for l in range(per_half):
                    lanes = slice(l * LANES, (l + 1) * LANES)
                    state[h * per_half + l, f, i] = total[f * size : (f + 1) * size, lanes]

    copies = functools.partial(
        make_copies, ORDERS, zsend, bufs, state, send_sem, recv_sem, nbrs
    )

    def start(c, stage):
        if ORDERS[c % len(ORDERS)][stage] == 2:
            for side in range(2):
                for f in range(2):
                    for i in range(ctrl):
                        rows = pl.ds(side * (ctrl - 1), ctrl, stride=ROWS)
                        zsend[c, side, f, i] = state[c, f, i, rows, :]
        for copy in copies(c, stage):
            copy.start()

    for h in range(halves):
        loads[h].wait()
        operate(h)
        if h == 0:
            pl.semaphore_wait(barrier, 6)
        for l in range(per_half):
            start(h * per_half + l, 0)

    index = lax.broadcasted_iota(jnp.int32, (ROWS, LANES), 0)
    index = jnp.maximum(ctrl - 1 - index, 0)
    flip_x, flip_y, flip_z = flips((ROWS, LANES))
    stores = []
    for c, stage in exchange_plan(chunks, per_half):
        d = ORDERS[c % len(ORDERS)][stage]
        for copy in copies(c, stage):
            copy.wait()
        for side in range(2):
            e = side * (ctrl - 1)
            for f in range(2):
                if d == 0:
                    state[c, f, e] += xbuf[c, side, f]
                    continue
                for i in range(ctrl):
                    if d == 1:
                        state[c, f, i, e * ROWS : e * ROWS + ctrl] += ybuf[c, side, f, i]
                    else:
                        rows = pl.ds(e, ctrl, stride=ROWS)
                        state[c, f, i, rows, :] = state[c, f, i, rows, :] + zbuf[c, side, f, i]
        if stage < 2:
            start(c, stage + 1)
            continue
        lanes = slice(c * LANES, (c + 1) * LANES)
        for f in range(2):
            for i in range(ctrl):
                for j in range(ctrl):
                    x = [
                        [state[c, f, ii, jj * ROWS : (jj + 1) * ROWS] for jj in (j, ctrl - 1 - j)]
                        for ii in (i, ctrl - 1 - i)
                    ]
                    x = [jnp.where(flip_y, y[1], y[0]) for y in x]
                    x = jnp.where(flip_x, x[1], x[0])
                    other = jnp.take_along_axis(x, index, axis=0, mode="promise_in_bounds")
                    turned[f, i, j, :, lanes] = jnp.where(flip_z, other, x)[0:ctrl]
            store = pltpu.make_async_copy(
                turned.at[f, :, :, :, lanes],
                (stiff_hbm, mass_hbm)[f].at[:, :, :, lanes],
                out_sem.at[c, f],
            )
            store.start()
            stores.append(store)
    for store in stores:
        store.wait()


ORDERS = ((0, 1, 2), (0, 1, 2), (0, 2, 1), (2, 1, 0))
WIRE = (1.23, 2.15, 2.15)
LATENCY = (2.2, 2.2, 3.4)


def exchange_plan(chunks, per_half):
    free = [0.0, 0.0, 0.0]
    heap, plan = [], []

    def send(time, chunk, stage):
        d = ORDERS[chunk % len(ORDERS)][stage]
        free[d] = max(free[d], time) + WIRE[d]
        heapq.heappush(heap, (free[d] + LATENCY[d], chunk, stage))

    for chunk in range(chunks):
        send(3.0 * (chunk // per_half), chunk, 0)
    now = 0.0
    while heap:
        time, chunk, stage = heapq.heappop(heap)
        now = max(now, time) + 0.3
        plan.append((chunk, stage))
        if stage < 2:
            send(now, chunk, stage + 1)
    return plan


def apply_patch(u, diag, off, weight, orient, values, slopes):
    quad, ctrl = values.shape
    vecs = u.shape[3]
    width = 2 * LANES
    halves = vecs // width
    chunks = vecs // LANES
    points = quad * quad
    size = ctrl * ROWS
    forward, backward = plane_tables(values, slopes)
    vmem = pl.BlockSpec(memory_space=pltpu.VMEM)
    hbm = pl.BlockSpec(memory_space=pl.ANY)
    f32 = jnp.float32
    return pl.pallas_call(
        functools.partial(patch_kernel, values, slopes),
        out_shape=[jax.ShapeDtypeStruct(u.shape, f32)] * 2,
        in_specs=[pl.BlockSpec(memory_space=pltpu.SMEM), hbm] + [vmem] * 5,
        out_specs=[hbm, hbm],
        scratch_shapes=[
            pltpu.VMEM((halves, ctrl, ctrl, ctrl, width), f32),
            pltpu.VMEM((2, ROWS, ROWS, width), f32),
            pltpu.VMEM((LANES, LANES), f32),
            pltpu.VMEM((7 * quad, points, LANES), f32),
            pltpu.VMEM((ctrl, 3 * points, width), f32),
            pltpu.VMEM((ctrl, 4 * points, width), f32),
            pltpu.VMEM((4 * size, 4 * points), jnp.bfloat16),
            pltpu.VMEM((chunks, 2, ctrl, size, LANES), f32),
            pltpu.VMEM((chunks, 2, 2, size, LANES), f32),
            pltpu.VMEM((chunks, 2, 2, ctrl, ctrl, LANES), f32),
            pltpu.VMEM((chunks, 2, 2, ctrl, ctrl, LANES), f32),
            pltpu.VMEM((chunks, 2, 2, ctrl, ctrl, LANES), f32),
            pltpu.VMEM((2, ctrl, ctrl, ctrl, vecs), f32),
            pltpu.SemaphoreType.DMA((halves,)),
            pltpu.SemaphoreType.DMA((chunks, 2)),
            pltpu.SemaphoreType.DMA((chunks, 3, 2)),
            pltpu.SemaphoreType.DMA((chunks, 3, 2)),
        ],
        compiler_params=pltpu.CompilerParams(collective_id=0, has_side_effects=True),
        name="apply_patch",
    )(orient, u, diag, off, weight, jnp.asarray(forward), jnp.asarray(backward))


def per_device(control_values, metric_diag, metric_off, mass_weight, orient):
    values, slopes = spline_tables(mass_weight.shape[0] // 2)
    return tuple(
        apply_patch(
            control_values, metric_diag, metric_off, mass_weight, orient.reshape(3), values, slopes
        )
    )


def solution(mesh):
    in_specs = (
        P("px", "py", "pz", None),
        P(None, "px", ("py", "pz")),
        P(None, "px", ("py", "pz")),
        P("px", ("py", "pz")),
        P("px", "py", "pz", None),
    )
    out_specs = (P("px", "py", "pz", None), P("px", "py", "pz", None))
    return jax.shard_map(
        per_device, mesh=mesh, in_specs=in_specs, out_specs=out_specs, check_vma=False
    )
```

profile of v0, /device:TPU:0, one launch (start us, length us, event | category | flops | bytes accessed | tf_op | source)
XLA Modules:
  0.0 28.4 jit_solution(3679477328804730341)
XLA Ops:
  0.6 24.7 %apply_patch.1 = (f32[7,7,7,512]{3,2,1,0:T(8,128)}, f32[7,7,7,512]{3,2,1,0:T(8,128)}) custom-call(s32[3]{0:T(128)} %bitcast.1, f32[7,7,7,512]{3,2,1,0:T(8,128)} %u_hbm.1, f32[3,8,64]{2,1,0:T(8,128)} %diag_ref.1, f32[3,8,64]{2,1,0:T(8,128)} %off_ref.1, f32[8,64]{1,0:T(8,128)} %weight_ref.1, bf16[192,192]{1,0:T(8,128)(2,1)} %constant.4.clone.fwd_ref, ...), custom_call_target="tpu_custom_call" | custom-call | tf_op jit(solution)/shard_map/apply_patch/pallas_call | solution.py:334
  25.4 0.0 copy-start
  25.4 2.1 %copy.11 = f32[7,7,7,512]{3,2,1,0:T(8,128)} copy(f32[7,7,7,512]{3,2,1,0:T(8,128)} %get-tuple-element.4) | data formatting | bytes 1404928
  27.5 0.0 copy-done
  27.5 0.9 %copy.12 = f32[7,7,7,512]{3,2,1,0:T(8,128)} copy(f32[7,7,7,512]{3,2,1,0:T(8,128)S(1)} %copy-done) | data formatting | bytes 1404928
Async XLA Ops:
  25.4 2.2 %copy-start = (f32[7,7,7,512]{3,2,1,0:T(8,128)S(1)}, f32[7,7,7,512]{3,2,1,0:T(8,128)}, u32[]{:S(2)}) copy-start(f32[7,7,7,512]{3,2,1,0:T(8,128)} %get-tuple-element.5) | copy-start | bytes 2107396
where the time goes:
time: 28.6 us; the launch traced here: 28.4 us
  Pallas kernels  24.7 us (86%)
  local copies, waits for them, and re-layouts  3.04 us (11%)
  between operations  0.65 us (2%)
    pallas_call x1, Pallas kernels, apply_patch(): pl.pallas_call(functools.partial(patch_kernel, values, slopes), out_shape...  24.7 us
    unnamed x4, local copies, waits for them, and re-layouts  3.04 us

commit v1 on v0

--- a/solution.py
+++ b/solution.py
@@ -239,19 +239,19 @@
         for copy in copies(c, stage):
             copy.start()
 
-    for h in range(halves):
-        loads[h].wait()
-        operate(h)
-        if h == 0:
-            pl.semaphore_wait(barrier, 6)
-        for l in range(per_half):
-            start(h * per_half + l, 0)
-
     index = lax.broadcasted_iota(jnp.int32, (ROWS, LANES), 0)
     index = jnp.maximum(ctrl - 1 - index, 0)
     flip_x, flip_y, flip_z = flips((ROWS, LANES))
     stores = []
     for c, stage in exchange_plan(chunks, per_half):
+        if stage < 0:
+            loads[c].wait()
+            operate(c)
+            if c == 0:
+                pl.semaphore_wait(barrier, 6)
+            for l in range(per_half):
+                start(c * per_half + l, 0)
+            continue
         d = ORDERS[c % len(ORDERS)][stage]
         for copy in copies(c, stage):
             copy.wait()
@@ -293,12 +293,14 @@
         store.wait()
 
 
-ORDERS = ((0, 1, 2), (0, 1, 2), (0, 2, 1), (2, 1, 0))
+ORDERS = ((0, 2, 1), (1, 0, 2), (0, 2, 1), (1, 0, 2))
 WIRE = (1.23, 2.15, 2.15)
 LATENCY = (2.2, 2.2, 3.4)
-
-
-def exchange_plan(chunks, per_half):
+COMPUTE = 1.7
+FOLD = 0.3
+
+
+def exchange_plan(chunks, per_part):
     free = [0.0, 0.0, 0.0]
     heap, plan = [], []
 
@@ -307,15 +309,22 @@
         free[d] = max(free[d], time) + WIRE[d]
         heapq.heappush(heap, (free[d] + LATENCY[d], chunk, stage))
 
-    for chunk in range(chunks):
-        send(3.0 * (chunk // per_half), chunk, 0)
+    def arrivals(now, limit):
+        while heap and heap[0][0] <= limit:
+            time, chunk, stage = heapq.heappop(heap)
+            now = max(now, time) + FOLD
+            plan.append((chunk, stage))
+            if stage < 2:
+                send(now, chunk, stage + 1)
+        return now
+
     now = 0.0
-    while heap:
-        time, chunk, stage = heapq.heappop(heap)
-        now = max(now, time) + 0.3
-        plan.append((chunk, stage))
-        if stage < 2:
-            send(now, chunk, stage + 1)
+    for part in range(chunks // per_part):
+        now = arrivals(now, now) + COMPUTE * per_part
+        plan.append((part, -1))
+        for chunk in range(part * per_part, (part + 1) * per_part):
+            send(now, chunk, 0)
+    arrivals(now, math.inf)
     return plan
 
 
@@ -360,13 +369,47 @@
     )(orient, u, diag, off, weight, jnp.asarray(forward), jnp.asarray(backward))
 
 
+def pass_kernel(stiff_in, mass_in, stiff_out, mass_out, buf, in_sem, out_sem):
+    pieces = [(f, i) for i in range(buf.shape[1]) for f in range(2)]
+    take = [
+        pltpu.make_async_copy((stiff_in, mass_in)[f].at[i], buf.at[f, i], in_sem.at[f, i])
+        for f, i in pieces
+    ]
+    give = [
+        pltpu.make_async_copy(buf.at[f, i], (stiff_out, mass_out)[f].at[i], out_sem.at[f, i])
+        for f, i in pieces
+    ]
+    for copy in take:
+        copy.start()
+    for first, second in zip(take, give):
+        first.wait()
+        second.start()
+    for copy in give:
+        copy.wait()
+
+
+def pass_through(stiff, mass):
+    hbm = pl.BlockSpec(memory_space=pl.ANY)
+    return pl.pallas_call(
+        pass_kernel,
+        out_shape=[jax.ShapeDtypeStruct(stiff.shape, stiff.dtype)] * 2,
+        in_specs=[hbm, hbm],
+        out_specs=[hbm, hbm],
+        scratch_shapes=[
+            pltpu.VMEM((2,) + stiff.shape, stiff.dtype),
+            pltpu.SemaphoreType.DMA((2, stiff.shape[0])),
+            pltpu.SemaphoreType.DMA((2, stiff.shape[0])),
+        ],
+        name="pass_through",
+    )(stiff, mass)
+
+
 def per_device(control_values, metric_diag, metric_off, mass_weight, orient):
     values, slopes = spline_tables(mass_weight.shape[0] // 2)
-    return tuple(
-        apply_patch(
-            control_values, metric_diag, metric_off, mass_weight, orient.reshape(3), values, slopes
-        )
-    )
+    stiff, mass = apply_patch(
+        control_values, metric_diag, metric_off, mass_weight, orient.reshape(3), values, slopes
+    )
+    return tuple(pass_through(stiff, mass))
 
 
 def solution(mesh):

time: 28.6 us -> 27.2 us (0.951)
  local copies, waits for them, and re-layouts: 3.04 us -> 0 us
  Pallas kernels: 24.7 us -> 26.4 us
    unnamed x4 -> x0, local copies, waits for them, and re-layouts: 3.04 us -> none
    pallas_call x0 -> x1, Pallas kernels: none -> 2.37 us  [pass_through(): pl.pallas_call(pass_kernel, out_shape=[jax.ShapeDtypeStruct(stiff.shape,...]
    pallas_call x1, Pallas kernels: 24.7 us -> 24 us  [apply_patch(): pl.pallas_call(functools.partial(patch_kernel, values, slopes), out_shape...]
where the time goes in v1:
time: 27.2 us; the launch traced here: 27 us
  Pallas kernels  26.4 us (97%)
  between operations  0.64 us (2%)
    pallas_call x1, Pallas kernels, apply_patch(): pl.pallas_call(functools.partial(patch_kernel, values, slopes), out_shape...  24 us
    pallas_call x1, Pallas kernels, pass_through(): pl.pallas_call(pass_kernel, out_shape=[jax.ShapeDtypeStruct(stiff.shape,...  2.37 us

profile of v1, /device:TPU:0, one launch (start us, length us, event | category | flops | bytes accessed | tf_op | source)
XLA Modules:
  0.0 27.0 jit_solution(11062845249760394465)
XLA Ops:
  0.6 24.0 %apply_patch.1 = (f32[7,7,7,512]{3,2,1,0:T(8,128)}, f32[7,7,7,512]{3,2,1,0:T(8,128)}) custom-call(s32[3]{0:T(128)} %bitcast.1, f32[7,7,7,512]{3,2,1,0:T(8,128)} %u_hbm.1, f32[3,8,64]{2,1,0:T(8,128)} %diag_ref.1, f32[3,8,64]{2,1,0:T(8,128)} %off_ref.1, f32[8,64]{1,0:T(8,128)} %weight_ref.1, bf16[192,192]{1,0:T(8,128)(2,1)} %constant.4.clone.fwd_ref, ...), custom_call_target="tpu_custom_call" | custom-call | tf_op jit(solution)/shard_map/apply_patch/pallas_call | solution.py:343
  24.7 2.4 %pass_through.1 = (f32[7,7,7,512]{3,2,1,0:T(8,128)}, f32[7,7,7,512]{3,2,1,0:T(8,128)}) custom-call(f32[7,7,7,512]{3,2,1,0:T(8,128)} %get-tuple-element.4.stiff_in, f32[7,7,7,512]{3,2,1,0:T(8,128)} %get-tuple-element.5.mass_in), custom_call_target="tpu_custom_call" | custom-call | tf_op jit(solution)/shard_map/pass_through/pallas_call | solution.py:393
